TPU v7x, 32 devices: a whole 2x2x4 slice. The times are simulated.
32 devices in a mesh: dom: 32 (over z, y, x, core).
Axes of the slice: x: 2, y: 2, z: 4, core: 2. Of those that a mesh axis runs over, the one named last changes fastest.
Arguments:
- concentration: float32 [1024, 128], P('dom'), may hold values from 0 to 1
- reaction_rate: float32 [1024, 128], P('dom'), may hold values from 0.5 to 4
- step_size: float32 [1], replicated, may hold values from 1 to 2
- block_values: float32 [1024, 5, 128, 128], P('dom'), may hold values from -40 to 48, as said below
- block_columns: int32 [1024, 5], P('dom'), may hold values from 0 to 95, as said below
- row_lengths: int32 [1024], P('dom'), may hold values from 2 to 5, as said below
- send_lists: int32 [32, 4, 16], P('dom'), may hold values from 0 to 31, as said below
Outputs:
- next_concentration: float32 [1024, 128], P('dom')
Inputs may be any that keep to these rules, and one draw needn't show every extreme that they name: `send_lists`: for every partition and offset index q (offsets -2, -1, +1, +2), 16 distinct local block indices. `block_columns`: slot 0 of a block row is the row's own local block; live slots name a local block (below 32) or a ghost slot 32 + q * 16 + g of a block that the partition at offset index q sends; slot 1 of local block row q, for q = 0..3, is a ghost slot of offset index q; slots at or past the row's length repeat the row's own local block. `row_lengths`: some block row has all 5 slots live. `block_values`: slot 0 of every block row holds 8 times the identity plus a full random block; the other slots hold full random blocks.
All inputs are finite; a program needn't handle non-finite values.
Results may differ from a plain program's by a relative error of at most 0.00016.
Values sent between devices are 32-bit elements; how exact they have to be, the bound alone decides.
A program may use at most 64 MiB of HBM per device.

v0:
```python
import functools

import jax
import jax.numpy as jnp
from jax import lax
from jax.experimental import pallas as pl
from jax.experimental.pallas import tpu as pltpu
from jax.sharding import PartitionSpec as P

KRYLOV = 3
RESTARTS = 2
OFFSETS = (-2, -1, 1, 2)
SHIFT = 8.0
SCALE = 4.0
GROUP = 8
EXCHANGES = 7
epsilon = 1e-06


def total(terms):
    result = terms[0]
    for term in terms[1:]:
        result = result + term
    return result


def quadratic(left, gram, right):
    return total(
        [a * total([gram[i][j] * b for j, b in enumerate(right)]) for i, a in enumerate(left)]
    )


def mapped_coefficients(c):
    result = [-SHIFT * c[0]]
    for i in range(1, len(c)):
        result.append(SCALE * c[i - 1] - SHIFT * c[i])
    result.append(SCALE * c[-1])
    return result


def subtract(a, weight, b):
    return [x - weight * b[i] if i < len(b) else x for i, x in enumerate(a)]


def multiply(a, b):
    size = len(a)
    result = []
    for i in range(size):
        row = []
        for j in range(size):
            terms = [
                a[i][k] * b[k][j]
                for k in range(size)
                if a[i][k] is not None and b[k][j] is not None
            ]
            row.append(total(terms) if terms else None)
        result.append(row)
    return result


def plus_identity(a, weight):
    return [
        [x * weight + 1.0 if i == j else x * weight for j, x in enumerate(row)]
        for i, row in enumerate(a)
    ]


def phi_column(hessenberg, substep):
    size = len(hessenberg)
    x = [
        [None if h is None else substep * h * (1.0 / 64.0) for h in row] for row in hessenberg
    ]
    one = jnp.ones_like(substep)
    zero = jnp.zeros_like(substep)
    series = [[one if i == j else zero for j in range(size)] for i in range(size)]
    for degree in range(12, 1, -1):
        series = plus_identity(multiply(x, series), 1.0 / degree)
    column = [series[i][0] * (1.0 / 64.0) for i in range(size)]
    power = plus_identity(multiply(x, series), 1.0)
    for turn in range(6):
        column = [
            total([power[i][k] * column[k] for k in range(size)]) + column[i] for i in range(size)
        ]
        if turn < 5:
            power = multiply(power, power)
    return column


def restart_coefficients(gram, substep):
    magnitude = jnp.sqrt(gram[0][0] + epsilon)
    basis = [[1.0 / magnitude]]
    hessenberg = [[None] * KRYLOV for _ in range(KRYLOV)]
    for column in range(KRYLOV):
        mapped = mapped_coefficients(basis[column])
        residue = mapped
        for k in range(column + 1):
            projection = quadratic(basis[k], gram, mapped)
            hessenberg[k][column] = projection
            residue = subtract(residue, projection, basis[k])
        if column + 1 < KRYLOV:
            squared = jnp.maximum(quadratic(residue, gram, residue), 0.0)
            length = jnp.sqrt(squared + epsilon)
            hessenberg[column + 1][column] = length
            inverse = 1.0 / length
            basis.append([x * inverse for x in residue])
    weights = phi_column(hessenberg, substep)
    factor = substep * magnitude
    return [
        factor * total([weights[k] * basis[k][i] for k in range(i, KRYLOV)]) for i in range(KRYLOV)
    ]


def kernel(n, *refs):
    operands, a_ref, y = refs[:6], refs[6], refs[7]
    staged = refs[8:14]
    step_ref, columns_ref, lengths_ref, lists_ref, c_ref, r_ref = staged
    scratch = list(refs[14:])
    stage_sem, table, a, local, mixed = scratch[:5]
    extended = scratch[5 : 5 + EXCHANGES]
    packets = scratch[5 + EXCHANGES : 5 + 2 * EXCHANGES]
    rest = scratch[5 + 2 * EXCHANGES :]
    sums, partial = rest[:RESTARTS], rest[RESTARTS : 2 * RESTARTS]
    load_sem, send_sem, recv_sem, sum_send, sum_recv = rest[2 * RESTARTS :]

    bdev, width = c_ref.shape
    slots = columns_ref.shape[0]
    gmax = lists_ref.shape[1]
    blank = bdev + len(OFFSETS) * gmax
    groups = bdev // GROUP
    me = lax.axis_index("dom")

    stages = [
        pltpu.make_async_copy(source, target, stage_sem.at[i])
        for i, (source, target) in enumerate(zip(operands, staged))
    ]
    for copy in stages:
        copy.start()
    loads = []
    for g in range(groups):
        rows = pl.ds(g * GROUP, GROUP)
        copy = pltpu.make_async_copy(a_ref.at[rows], a.at[rows], load_sem.at[g])
        copy.start()
        loads.append(copy)

    barrier = pltpu.get_barrier_semaphore()

    def greet(d, carry):
        pl.semaphore_signal(
            barrier,
            inc=1,
            device_id=(lax.rem(me + d, n),),
            device_id_type=pl.DeviceIdType.MESH,
        )
        return carry

    lax.fori_loop(1, n, greet, 0)
    for copy in stages:
        copy.wait()

    def copies(e):
        return [
            pltpu.make_async_remote_copy(
                src_ref=packets[e].at[q],
                dst_ref=extended[e].at[pl.ds(bdev + q * gmax, gmax)],
                send_sem=send_sem.at[e, q],
                recv_sem=recv_sem.at[e, q],
                device_id=(lax.rem(me + offset + n, n),),
                device_id_type=pl.DeviceIdType.MESH,
            )
            for q, offset in enumerate(OFFSETS)
        ]

    def pack(e, field):
        local[...] = field
        for q in range(len(OFFSETS)):
            for g in range(gmax):
                packets[e][q, g : g + 1, :] = local[pl.ds(lists_ref[q, g], 1), :]

    def send(e):
        for copy in copies(e):
            copy.start()
        extended[e][0:bdev, :] = local[...]
        extended[e][blank:, :] = jnp.zeros((8, width), jnp.float32)

    def arrive(e):
        for copy in copies(e):
            copy.wait_recv()

    row_of = lax.broadcasted_iota(jnp.int32, (GROUP, 2 * width), 0)

    def group_product(source, g):
        result = None
        for i in range(GROUP):
            row = g * GROUP + i
            acc = None
            for t in range(slots):
                term = a[row, t] * source[pl.ds(table[row * slots + t], 1), :]
                acc = term if acc is None else acc + term
            high = acc.astype(jnp.bfloat16)
            low = (acc - high.astype(jnp.float32)).astype(jnp.bfloat16)
            both = jnp.concatenate([high, low], axis=1)
            pick = jnp.where(row_of == i, 1.0, 0.0).astype(jnp.bfloat16)
            part = lax.dot_general(
                pick, both, (((1,), (1,)), ((), ())), preferred_element_type=jnp.float32
            )
            result = part if result is None else result + part
        return result

    def operator(source):
        return jnp.concatenate([group_product(source, g) for g in range(groups)], axis=0)

    lane = lax.broadcasted_iota(jnp.int32, (1, width), 1)

    def dots(row, fields, last):
        for i in range(last + 1):
            folded = jnp.sum(fields[i] * fields[last], axis=0, keepdims=True)
            value = jnp.sum(folded, axis=1, keepdims=True)
            row = jnp.where(lane == last * (last + 1) // 2 + i, value, row)
        return row

    def send_sums(turn, row):
        partial[turn][...] = row
        sums[turn][me] = row

        def one(d, carry):
            pltpu.make_async_remote_copy(
                src_ref=partial[turn],
                dst_ref=sums[turn].at[me],
                send_sem=sum_send.at[turn],
                recv_sem=sum_recv.at[turn],
                device_id=(lax.rem(me + d, n),),
                device_id_type=pl.DeviceIdType.MESH,
            ).start()
            return carry

        lax.fori_loop(1, n, one, 0)

    def gather_sums(turn, count):
        others = sums[turn].at[pl.ds(0, n - 1)]
        pltpu.make_async_copy(others, others, sum_recv.at[turn]).wait()
        row = jnp.sum(sums[turn][...], axis=0)
        gram = [[None] * count for _ in range(count)]
        for j in range(count):
            for i in range(j + 1):
                index = j * (j + 1) // 2 + i
                value = jnp.sum(jnp.where(lane == index, row, 0.0), axis=1, keepdims=True)
                gram[i][j] = gram[j][i] = jnp.broadcast_to(value, (8, width))
        return gram

    def combine(weights, fields):
        return total(
            [
                jnp.concatenate([w] * (f.shape[0] // 8), axis=0) * f
                for w, f in zip(weights, fields)
            ]
        )

    concentration = c_ref[...]
    rate = r_ref[...]
    shifted = (rate * (1.0 - 2.0 * concentration) + SHIFT) * (1.0 / SCALE)
    substep = jnp.full((8, width), step_ref[0] * (1.0 / RESTARTS), jnp.float32)

    def apply(source, field):
        return shifted * field - operator(source) * (1.0 / SCALE)

    pack(0, concentration)
    pl.semaphore_wait(barrier, n - 1)
    send(0)

    def fill(row, carry):
        length = lengths_ref[row]
        for t in range(slots):
            table[row * slots + t] = jnp.where(t < length, columns_ref[t, row], blank)
        return carry

    lax.fori_loop(0, bdev, fill, 0)
    for copy in loads:
        copy.wait()
    arrive(0)
    field = rate * concentration * (1.0 - concentration) - operator(extended[0])

    fields = [field]
    row = jnp.zeros((1, width), jnp.float32)
    for j in range(KRYLOV):
        pack(1 + j, field)
        send(1 + j)
        row = dots(row, fields, j)
        arrive(1 + j)
        field = apply(extended[1 + j], field)
        fields.append(field)

    e = KRYLOV + 1
    pack(e, field)
    send(e)
    send_sums(0, dots(row, fields, KRYLOV))
    arrive(e)
    field = apply(extended[e], field)
    fields.append(field)
    e = KRYLOV + 2
    pack(e, field)
    send(e)
    d = restart_coefficients(gather_sums(0, KRYLOV + 1), substep)
    s = mapped_coefficients(d)
    s[0] = s[0] + 1.0
    start = combine(s, fields[:-1])
    field = combine(s, fields[1:])
    base = concentration + combine(d, fields[:KRYLOV])
    mixed[0:bdev, :] = field
    mixed[blank:, :] = jnp.zeros((8, width), jnp.float32)
    fields = [start, field]
    row = jnp.zeros((1, width), jnp.float32)
    row = dots(dots(row, fields, 0), fields, 1)
    arrive(e)
    mixed[bdev:blank, :] = combine(
        s, [extended[2 + j][bdev:blank, :] for j in range(KRYLOV + 1)]
    )
    field = apply(mixed, field)
    fields.append(field)
    for j in range(2, KRYLOV):
        e = KRYLOV + 1 + j
        pack(e, field)
        send(e)
        row = dots(row, fields, j)
        arrive(e)
        field = apply(extended[e], field)
        fields.append(field)
    send_sums(1, dots(row, fields, KRYLOV))
    d = restart_coefficients(gather_sums(1, KRYLOV + 1), substep)
    y[...] = base + combine(d, fields[:KRYLOV])

    for e in range(EXCHANGES):
        for copy in copies(e):
            copy.wait_send()
    for turn in range(RESTARTS):
        others = sums[turn].at[pl.ds(0, n - 1)]
        pltpu.make_async_copy(others, others, sum_send.at[turn]).wait()


def solution(mesh):
    n = mesh.shape["dom"]

    def shards(c, r, step, values, columns, lengths, lists):
        bdev, width = c.shape
        slots = columns.shape[1]
        sides, gmax = lists.shape[1:]
        tall = bdev + sides * gmax + 8
        f32 = jnp.float32
        held = pl.BlockSpec(memory_space=pltpu.HBM)
        vmem = pl.BlockSpec(memory_space=pltpu.VMEM)
        return pl.pallas_call(
            functools.partial(kernel, n),
            out_shape=jax.ShapeDtypeStruct((bdev, width), f32),
            in_specs=[held] * 7,
            out_specs=vmem,
            scratch_shapes=[
                pltpu.SMEM((1,), f32),
                pltpu.SMEM((slots, bdev), jnp.int32),
                pltpu.SMEM((bdev,), jnp.int32),
                pltpu.SMEM((sides, gmax), jnp.int32),
                pltpu.VMEM((bdev, width), f32),
                pltpu.VMEM((bdev, width), f32),
                pltpu.SemaphoreType.DMA((6,)),
                pltpu.SMEM((bdev * slots,), jnp.int32),
                pltpu.VMEM((bdev, slots, width, width), f32),
                pltpu.VMEM((bdev, width), f32),
                pltpu.VMEM((tall, width), f32),
            ]
            + [pltpu.VMEM((tall, width), f32)] * EXCHANGES
            + [pltpu.VMEM((sides, gmax, width), f32)] * EXCHANGES
            + [pltpu.VMEM((n, 1, width), f32)] * RESTARTS
            + [pltpu.VMEM((1, width), f32)] * RESTARTS
            + [
                pltpu.SemaphoreType.DMA((bdev // GROUP,)),
                pltpu.SemaphoreType.DMA((EXCHANGES, sides)),
                pltpu.SemaphoreType.DMA((EXCHANGES, sides)),
                pltpu.SemaphoreType.DMA((RESTARTS,)),
                pltpu.SemaphoreType.DMA((RESTARTS,)),
            ],
            compiler_params=pltpu.CompilerParams(
                collective_id=0, has_side_effects=True, vmem_limit_bytes=67043328
            ),
        )(step, columns.T, lengths, lists[0], c, r, values)

    placed = (
        P("dom", None),
        P("dom", None),
        P(),
        P("dom", None, None, None),
        P("dom", None),
        P("dom"),
        P("dom", None, None),
    )
    return jax.shard_map(
        shards, mesh=mesh, in_specs=placed, out_specs=P("dom", None), check_vma=False
    )
```

profile of v0, /device:TPU:0, one launch (start us, length us, event | category | flops | bytes accessed | tf_op | source)
XLA Modules:
  0.0 53.4 jit_solution(7056533401934156488)
XLA Ops:
  0.7 51.4 %shard_map.73 = f32[32,128]{1,0:T(8,128)} custom-call(f32[1]{0:T(128)S(6)} %copy.9.refs_0_, s32[5,32]{1,0:T(8,128)} %bitcast.2, s32[32]{0:T(128)} %refs_2_.1, s32[4,16]{1,0:T(4,128)} %bitcast.3, f32[32,128]{1,0:T(8,128)} %refs_4_.1, f32[32,128]{1,0:T(8,128)} %refs_5_.1, f32[32,5,128,128]{3,2,1,0:T(8,128)} %refs_6_.1), custom_call_target="tpu_custom_call" | custom-call | tf_op jit(solution)/shard_map/pallas_call | solution.py:350
  52.1 1.3 %copy.10 = f32[32,128]{1,0:T(8,128)} copy(f32[32,128]{1,0:T(8,128)} %shard_map.73) | data formatting | bytes 32768
where the time goes:
time: 53.7 us; the launch traced here: 53.4 us
  Pallas kernels  51.4 us (96%)
  local copies, waits for them, and re-layouts  1.32 us (2%)
  between operations  0.66 us (1%)
    pallas_call x1, Pallas kernels, shards(): pl.pallas_call(functools.partial(kernel, n), out_shape=jax.ShapeDtypeStru...  51.4 us
    unnamed x1, local copies, waits for them, and re-layouts  1.32 us

commit v1 on v0

--- a/solution.py
+++ b/solution.py
@@ -12,7 +12,7 @@
 OFFSETS = (-2, -1, 1, 2)
 SHIFT = 8.0
 SCALE = 4.0
-GROUP = 8
+TILE = 8
 EXCHANGES = 7
 epsilon = 1e-06
 
@@ -110,37 +110,38 @@
     ]
 
 
+def merge_rows(parts):
+    sublane = lax.broadcasted_iota(jnp.int32, parts[0].shape, 0)
+    distance = 1
+    while len(parts) > 1:
+        first = (sublane // distance) % 2 == 0
+        parts = [
+            jnp.where(first, u, v)
+            + pltpu.roll(jnp.where(first, v, u), TILE - distance, 0)
+            for u, v in zip(parts[0::2], parts[1::2])
+        ]
+        distance *= 2
+    return parts[0]
+
+
 def kernel(n, *refs):
     operands, a_ref, y = refs[:6], refs[6], refs[7]
     staged = refs[8:14]
     step_ref, columns_ref, lengths_ref, lists_ref, c_ref, r_ref = staged
     scratch = list(refs[14:])
-    stage_sem, table, a, local, mixed = scratch[:5]
-    extended = scratch[5 : 5 + EXCHANGES]
-    packets = scratch[5 + EXCHANGES : 5 + 2 * EXCHANGES]
-    rest = scratch[5 + 2 * EXCHANGES :]
+    stage_sem, inverse, order, table, places, a, local, rates, mixed = scratch[:9]
+    scratch = scratch[9:]
+    extended = scratch[:EXCHANGES]
+    packets = scratch[EXCHANGES : 2 * EXCHANGES]
+    rest = scratch[2 * EXCHANGES :]
     sums, partial = rest[:RESTARTS], rest[RESTARTS : 2 * RESTARTS]
     load_sem, send_sem, recv_sem, sum_send, sum_recv = rest[2 * RESTARTS :]
 
     bdev, width = c_ref.shape
     slots = columns_ref.shape[0]
-    gmax = lists_ref.shape[1]
-    blank = bdev + len(OFFSETS) * gmax
-    groups = bdev // GROUP
+    sides, gmax = lists_ref.shape
+    blank = bdev + sides * gmax
     me = lax.axis_index("dom")
-
-    stages = [
-        pltpu.make_async_copy(source, target, stage_sem.at[i])
-        for i, (source, target) in enumerate(zip(operands, staged))
-    ]
-    for copy in stages:
-        copy.start()
-    loads = []
-    for g in range(groups):
-        rows = pl.ds(g * GROUP, GROUP)
-        copy = pltpu.make_async_copy(a_ref.at[rows], a.at[rows], load_sem.at[g])
-        copy.start()
-        loads.append(copy)
 
     barrier = pltpu.get_barrier_semaphore()
 
@@ -153,61 +154,145 @@
         )
         return carry
 
+    stages = [
+        pltpu.make_async_copy(source, target, stage_sem.at[i])
+        for i, (source, target) in enumerate(zip(operands, staged))
+    ]
+    for copy in stages:
+        copy.start()
     lax.fori_loop(1, n, greet, 0)
+    loads = []
+    for g in range(0, bdev, TILE):
+        rows = pl.ds(g, TILE)
+        copy = pltpu.make_async_copy(a_ref.at[rows], a.at[rows], load_sem.at[g // TILE])
+        copy.start()
+        loads.append(copy)
     for copy in stages:
         copy.wait()
 
-    def copies(e):
+    lead = (sides - 1) * lax.div(2 * me, n)
+
+    def side(j):
+        q = lax.rem(lead + j, sides)
+        return q, q - 2 + lax.div(q, 2)
+
+    def remote(e, q, offset, slot, source):
+        return pltpu.make_async_remote_copy(
+            src_ref=source,
+            dst_ref=extended[e].at[pl.ds(bdev + q * gmax, gmax)],
+            send_sem=send_sem.at[e, slot],
+            recv_sem=recv_sem.at[e, q],
+            device_id=(lax.rem(me + offset + n, n),),
+            device_id_type=pl.DeviceIdType.MESH,
+        )
+
+    def first_copies():
         return [
-            pltpu.make_async_remote_copy(
-                src_ref=packets[e].at[q],
-                dst_ref=extended[e].at[pl.ds(bdev + q * gmax, gmax)],
-                send_sem=send_sem.at[e, q],
-                recv_sem=recv_sem.at[e, q],
-                device_id=(lax.rem(me + offset + n, n),),
-                device_id_type=pl.DeviceIdType.MESH,
+            remote(0, q, offset, q, packets[0].at[q]) for q, offset in enumerate(OFFSETS)
+        ]
+
+    def copy_of(e, j):
+        q, offset = side(j)
+        source = packets[e].at[j] if j else extended[e].at[pl.ds(0, gmax)]
+        return remote(e, q, offset, j, source)
+
+    def send_lead(e):
+        copy_of(e, 0).start()
+
+    def send_rest(e):
+        for j in range(1, sides):
+            q, _ = side(j)
+            for g in range(gmax):
+                packets[e][j, g : g + 1, :] = local[pl.ds(places[q * gmax + g], 1), :]
+        for j in range(1, sides):
+            copy_of(e, j).start()
+
+    def arrive(e):
+        for q in range(sides):
+            remote(e, q, 0, q, extended[e].at[pl.ds(0, gmax)]).wait_recv()
+
+    def clear(target):
+        target[blank:, :] = jnp.zeros((8, width), jnp.float32)
+
+    for q in range(sides):
+        for g in range(gmax):
+            packets[0][q, g : g + 1, :] = c_ref[pl.ds(lists_ref[q, g], 1), :]
+    pl.semaphore_wait(barrier, n - 1)
+    for copy in first_copies():
+        copy.start()
+
+    def fill_inverse(row, carry):
+        hit = jnp.int32(0)
+        below = jnp.int32(0)
+        for i in range(gmax):
+            listed = lists_ref[lead, i]
+            hit = jnp.where(listed == row, i + 1, hit)
+            below = below + jnp.where(listed < row, 1, 0)
+        inverse[row] = jnp.where(hit > 0, hit - 1, gmax + row - below)
+        return carry
+
+    lax.fori_loop(0, bdev, fill_inverse, 0)
+
+    def fill_lead(i, carry):
+        order[i] = lists_ref[lead, i]
+        for q in range(sides):
+            places[q * gmax + i] = inverse[lists_ref[q, i]]
+        return carry
+
+    lax.fori_loop(0, gmax, fill_lead, 0)
+
+    def fill_others(i, carry):
+        row = jnp.int32(0)
+        for r in range(bdev):
+            row = row + jnp.where(inverse[r] == i, r, 0)
+        order[i] = row
+        return carry
+
+    lax.fori_loop(gmax, bdev, fill_others, 0)
+
+    def fill_table(i, carry):
+        row = order[i]
+        length = lengths_ref[row]
+        for t in range(1, slots):
+            column = columns_ref[t, row]
+            place = jnp.where(column < bdev, inverse[jnp.minimum(column, bdev - 1)], column)
+            table[i * slots + t] = jnp.where(t < length, place, blank)
+        return carry
+
+    lax.fori_loop(0, bdev, fill_table, 0)
+
+    def rowsum(products):
+        turned = products.T
+        return total([turned[k : k + TILE, :] for k in range(0, width, TILE)])
+
+    def own_product(x):
+        result = []
+        for g in range(0, bdev, TILE):
+            result.append(
+                merge_rows(
+                    [rowsum(a[order[i], 0] * x[i : i + 1, :]) for i in range(g, g + TILE)]
+                )
             )
-            for q, offset in enumerate(OFFSETS)
-        ]
-
-    def pack(e, field):
-        local[...] = field
-        for q in range(len(OFFSETS)):
-            for g in range(gmax):
-                packets[e][q, g : g + 1, :] = local[pl.ds(lists_ref[q, g], 1), :]
-
-    def send(e):
-        for copy in copies(e):
-            copy.start()
-        extended[e][0:bdev, :] = local[...]
-        extended[e][blank:, :] = jnp.zeros((8, width), jnp.float32)
-
-    def arrive(e):
-        for copy in copies(e):
-            copy.wait_recv()
-
-    row_of = lax.broadcasted_iota(jnp.int32, (GROUP, 2 * width), 0)
-
-    def group_product(source, g):
-        result = None
-        for i in range(GROUP):
-            row = g * GROUP + i
-            acc = None
-            for t in range(slots):
-                term = a[row, t] * source[pl.ds(table[row * slots + t], 1), :]
-                acc = term if acc is None else acc + term
-            high = acc.astype(jnp.bfloat16)
-            low = (acc - high.astype(jnp.float32)).astype(jnp.bfloat16)
-            both = jnp.concatenate([high, low], axis=1)
-            pick = jnp.where(row_of == i, 1.0, 0.0).astype(jnp.bfloat16)
-            part = lax.dot_general(
-                pick, both, (((1,), (1,)), ((), ())), preferred_element_type=jnp.float32
-            )
-            result = part if result is None else result + part
-        return result
-
-    def operator(source):
-        return jnp.concatenate([group_product(source, g) for g in range(groups)], axis=0)
+        return jnp.concatenate(result, axis=0)
+
+    def other_product(source, start, stop):
+        result = []
+        for g in range(start, stop, TILE):
+            parts = []
+            for i in range(g, g + TILE):
+                row = order[i]
+                parts.append(
+                    rowsum(
+                        total(
+                            [
+                                a[row, t] * source[pl.ds(table[i * slots + t], 1), :]
+                                for t in range(1, slots)
+                            ]
+                        )
+                    )
+                )
+            result.append(merge_rows(parts))
+        return jnp.concatenate(result, axis=0)
 
     lane = lax.broadcasted_iota(jnp.int32, (1, width), 1)
 
@@ -255,50 +340,59 @@
             ]
         )
 
-    concentration = c_ref[...]
-    rate = r_ref[...]
+    for i in range(bdev):
+        row = order[i]
+        local[i : i + 1, :] = c_ref[pl.ds(row, 1), :]
+        rates[i : i + 1, :] = r_ref[pl.ds(row, 1), :]
+    concentration = local[...]
+    rate = rates[...]
     shifted = (rate * (1.0 - 2.0 * concentration) + SHIFT) * (1.0 / SCALE)
     substep = jnp.full((8, width), step_ref[0] * (1.0 / RESTARTS), jnp.float32)
-
-    def apply(source, field):
-        return shifted * field - operator(source) * (1.0 / SCALE)
-
-    pack(0, concentration)
-    pl.semaphore_wait(barrier, n - 1)
-    send(0)
-
-    def fill(row, carry):
-        length = lengths_ref[row]
-        for t in range(slots):
-            table[row * slots + t] = jnp.where(t < length, columns_ref[t, row], blank)
-        return carry
-
-    lax.fori_loop(0, bdev, fill, 0)
+    for e in range(EXCHANGES):
+        clear(extended[e])
+    clear(mixed)
+
+    def finish(e, source, known, scale):
+        parts = []
+        for start in range(0, bdev, gmax):
+            rows = slice(start, start + gmax)
+            part = known[rows] - scale * other_product(source, start, start + gmax)
+            parts.append(part)
+            if e is not None:
+                extended[e][rows, :] = part
+                local[rows, :] = part
+                if start == 0:
+                    send_lead(e)
+        if e is not None:
+            send_rest(e)
+        return jnp.concatenate(parts, axis=0)
+
+    def known_part(field):
+        return shifted * field - own_product(field) * (1.0 / SCALE)
+
+    extended[0][0:bdev, :] = concentration
     for copy in loads:
         copy.wait()
+    known = rate * concentration * (1.0 - concentration) - own_product(concentration)
     arrive(0)
-    field = rate * concentration * (1.0 - concentration) - operator(extended[0])
+    field = finish(1, extended[0], known, 1.0)
 
     fields = [field]
     row = jnp.zeros((1, width), jnp.float32)
     for j in range(KRYLOV):
-        pack(1 + j, field)
-        send(1 + j)
         row = dots(row, fields, j)
+        known = known_part(field)
         arrive(1 + j)
-        field = apply(extended[1 + j], field)
+        field = finish(2 + j, extended[1 + j], known, 1.0 / SCALE)
         fields.append(field)
 
     e = KRYLOV + 1
-    pack(e, field)
-    send(e)
     send_sums(0, dots(row, fields, KRYLOV))
+    known = known_part(field)
     arrive(e)
-    field = apply(extended[e], field)
+    field = finish(e + 1, extended[e], known, 1.0 / SCALE)
     fields.append(field)
     e = KRYLOV + 2
-    pack(e, field)
-    send(e)
     d = restart_coefficients(gather_sums(0, KRYLOV + 1), substep)
     s = mapped_coefficients(d)
     s[0] = s[0] + 1.0
@@ -306,7 +400,7 @@
     field = combine(s, fields[1:])
     base = concentration + combine(d, fields[:KRYLOV])
     mixed[0:bdev, :] = field
-    mixed[blank:, :] = jnp.zeros((8, width), jnp.float32)
+    known = known_part(field)
     fields = [start, field]
     row = jnp.zeros((1, width), jnp.float32)
     row = dots(dots(row, fields, 0), fields, 1)
@@ -314,23 +408,27 @@
     mixed[bdev:blank, :] = combine(
         s, [extended[2 + j][bdev:blank, :] for j in range(KRYLOV + 1)]
     )
-    field = apply(mixed, field)
-    fields.append(field)
-    for j in range(2, KRYLOV):
+    source = mixed
+    for j in range(2, KRYLOV + 1):
         e = KRYLOV + 1 + j
-        pack(e, field)
-        send(e)
-        row = dots(row, fields, j)
-        arrive(e)
-        field = apply(extended[e], field)
+        field = finish(e if j < KRYLOV else None, source, known, 1.0 / SCALE)
         fields.append(field)
+        if j < KRYLOV:
+            row = dots(row, fields, j)
+            known = known_part(field)
+            arrive(e)
+            source = extended[e]
     send_sums(1, dots(row, fields, KRYLOV))
     d = restart_coefficients(gather_sums(1, KRYLOV + 1), substep)
-    y[...] = base + combine(d, fields[:KRYLOV])
-
-    for e in range(EXCHANGES):
-        for copy in copies(e):
-            copy.wait_send()
+    local[...] = base + combine(d, fields[:KRYLOV])
+    for r in range(bdev):
+        y[r : r + 1, :] = local[pl.ds(inverse[r], 1), :]
+
+    for copy in first_copies():
+        copy.wait_send()
+    for e in range(1, EXCHANGES):
+        for j in range(sides):
+            copy_of(e, j).wait_send()
     for turn in range(RESTARTS):
         others = sums[turn].at[pl.ds(0, n - 1)]
         pltpu.make_async_copy(others, others, sum_send.at[turn]).wait()
@@ -360,8 +458,12 @@
                 pltpu.VMEM((bdev, width), f32),
                 pltpu.VMEM((bdev, width), f32),
                 pltpu.SemaphoreType.DMA((6,)),
+                pltpu.SMEM((bdev,), jnp.int32),
+                pltpu.SMEM((bdev,), jnp.int32),
                 pltpu.SMEM((bdev * slots,), jnp.int32),
+                pltpu.SMEM((sides * gmax,), jnp.int32),
                 pltpu.VMEM((bdev, slots, width, width), f32),
+                pltpu.VMEM((bdev, width), f32),
                 pltpu.VMEM((bdev, width), f32),
                 pltpu.VMEM((tall, width), f32),
             ]
@@ -370,7 +472,7 @@
             + [pltpu.VMEM((n, 1, width), f32)] * RESTARTS
             + [pltpu.VMEM((1, width), f32)] * RESTARTS
             + [
-                pltpu.SemaphoreType.DMA((bdev // GROUP,)),
+                pltpu.SemaphoreType.DMA((bdev // TILE,)),
                 pltpu.SemaphoreType.DMA((EXCHANGES, sides)),
                 pltpu.SemaphoreType.DMA((EXCHANGES, sides)),
                 pltpu.SemaphoreType.DMA((RESTARTS,)),

time: 53.7 us -> 49.3 us (0.918)
  Pallas kernels: 51.4 us -> 47.1 us
    pallas_call x1, Pallas kernels: 51.4 us -> 47.1 us  [shards(): pl.pallas_call(functools.partial(kernel, n), out_shape=jax.ShapeDtypeStru...]
where the time goes in v1:
time: 49.3 us; the launch traced here: 49.1 us
  Pallas kernels  47.1 us (96%)
  local copies, waits for them, and re-layouts  1.32 us (3%)
  between operations  0.66 us (1%)
    pallas_call x1, Pallas kernels, shards(): pl.pallas_call(functools.partial(kernel, n), out_shape=jax.ShapeDtypeStru...  47.1 us
    unnamed x1, local copies, waits for them, and re-layouts  1.32 us

profile of v1, /device:TPU:0, one launch (start us, length us, event | category | flops | bytes accessed | tf_op | source)
XLA Modules:
  0.0 49.1 jit_solution(5595570929703492770)
XLA Ops:
  0.7 47.1 %shard_map.73 = f32[32,128]{1,0:T(8,128)} custom-call(f32[1]{0:T(128)S(6)} %copy.9.refs_0_, s32[5,32]{1,0:T(8,128)} %bitcast.2, s32[32]{0:T(128)} %refs_2_.1, s32[4,16]{1,0:T(4,128)} %bitcast.3, f32[32,128]{1,0:T(8,128)} %refs_4_.1, f32[32,128]{1,0:T(8,128)} %refs_5_.1, f32[32,5,128,128]{3,2,1,0:T(8,128)} %refs_6_.1), custom_call_target="tpu_custom_call" | custom-call | tf_op jit(solution)/shard_map/pallas_call | solution.py:448
  47.8 1.3 %copy.10 = f32[32,128]{1,0:T(8,128)} copy(f32[32,128]{1,0:T(8,128)} %shard_map.73) | data formatting | bytes 32768

commit v2 on v1

--- a/solution.py
+++ b/solution.py
@@ -479,9 +479,9 @@
                 pltpu.SemaphoreType.DMA((RESTARTS,)),
             ],
             compiler_params=pltpu.CompilerParams(
-                collective_id=0, has_side_effects=True, vmem_limit_bytes=67043328
+                collective_id=0, has_side_effects=True, vmem_limit_bytes=20 << 20
             ),
-        )(step, columns.T, lengths, lists[0], c, r, values)
+        )(step, *[pltpu.with_memory_space_constraint(x, pltpu.HBM) for x in (columns.T, lengths, lists[0], c, r, values)])
 
     placed = (
         P("dom", None),

time: 49.3 us -> 47.9 us (0.972)
  local copies, waits for them, and re-layouts: 1.32 us -> 0.61 us
  Pallas kernels: 47.1 us -> 46.5 us
    unnamed x1, local copies, waits for them, and re-layouts: 1.32 us -> 0.61 us
    pallas_call x1, Pallas kernels: 47.1 us -> 46.5 us  [shards(): pl.pallas_call(functools.partial(kernel, n), out_shape=jax.ShapeDtypeStru...]
where the time goes in v2:
time: 47.9 us; the launch traced here: 47.8 us
  Pallas kernels  46.5 us (97%)
  between operations  0.66 us (1%)
  local copies, waits for them, and re-layouts  0.61 us (1%)
    pallas_call x1, Pallas kernels, shards(): pl.pallas_call(functools.partial(kernel, n), out_shape=jax.ShapeDtypeStru...  46.5 us

profile of v2, /device:TPU:0, one launch (start us, length us, event | category | flops | bytes accessed | tf_op | source)
XLA Modules:
  0.0 47.8 jit_solution(7243012594401330715)
XLA Ops:
  0.7 46.5 %shard_map.73 = f32[32,128]{1,0:T(8,128)S(1)} custom-call(f32[1]{0:T(128)S(6)} %copy.9.refs_0_, s32[5,32]{1,0:T(8,128)} %bitcast.2, s32[32]{0:T(128)} %refs_2_.1, s32[4,16]{1,0:T(4,128)} %bitcast.3, f32[32,128]{1,0:T(8,128)} %refs_4_.1, f32[32,128]{1,0:T(8,128)} %refs_5_.1, f32[32,5,128,128]{3,2,1,0:T(8,128)} %refs_6_.1), custom_call_target="tpu_custom_call" | custom-call | tf_op jit(solution)/shard_map/pallas_call | solution.py:448
  47.2 0.6 %copy.10 = f32[32,128]{1,0:T(8,128)} copy(f32[32,128]{1,0:T(8,128)S(1)} %shard_map.73) | data formatting | bytes 32768

commit v3 on v2

--- a/solution.py
+++ b/solution.py
@@ -14,6 +14,7 @@
 SCALE = 4.0
 TILE = 8
 EXCHANGES = 7
+UP = 2
 epsilon = 1e-06
 
 
@@ -130,7 +131,8 @@
     step_ref, columns_ref, lengths_ref, lists_ref, c_ref, r_ref = staged
     scratch = list(refs[14:])
     stage_sem, inverse, order, table, places, a, local, rates, mixed = scratch[:9]
-    scratch = scratch[9:]
+    columns_v, lengths_v, natural, z, w, w_send, w_recv = scratch[9:16]
+    scratch = scratch[16:]
     extended = scratch[:EXCHANGES]
     packets = scratch[EXCHANGES : 2 * EXCHANGES]
     rest = scratch[2 * EXCHANGES :]
@@ -156,7 +158,9 @@
 
     stages = [
         pltpu.make_async_copy(source, target, stage_sem.at[i])
-        for i, (source, target) in enumerate(zip(operands, staged))
+        for i, (source, target) in enumerate(
+            [*zip(operands, staged), (operands[1], columns_v), (operands[2], lengths_v)]
+        )
     ]
     for copy in stages:
         copy.start()
@@ -199,11 +203,40 @@
     def send_lead(e):
         copy_of(e, 0).start()
 
+    def pack(e, j, q):
+        for g in range(gmax):
+            packets[e][j, g : g + 1, :] = local[pl.ds(places[q * gmax + g], 1), :]
+
+    def last_copies():
+        return [
+            remote(EXCHANGES - 1, q, OFFSETS[q], q, packets[EXCHANGES - 1].at[q])
+            for q in range(UP, sides)
+        ]
+
+    def send_last():
+        for q in range(UP, sides):
+            pack(EXCHANGES - 1, q, q)
+        for copy in last_copies():
+            copy.start()
+        for q in range(UP):
+            pack(EXCHANGES - 1, q, q)
+
+    def z_copies(i):
+        return [
+            pltpu.make_async_remote_copy(
+                src_ref=z.at[i, pl.ds(bdev + q * gmax, gmax)],
+                dst_ref=w.at[i, q],
+                send_sem=w_send.at[i, q],
+                recv_sem=w_recv.at[i, q],
+                device_id=(lax.rem(me - OFFSETS[q] + n, n),),
+                device_id_type=pl.DeviceIdType.MESH,
+            )
+            for q in range(UP)
+        ]
+
     def send_rest(e):
         for j in range(1, sides):
-            q, _ = side(j)
-            for g in range(gmax):
-                packets[e][j, g : g + 1, :] = local[pl.ds(places[q * gmax + g], 1), :]
+            pack(e, j, side(j)[0])
         for j in range(1, sides):
             copy_of(e, j).start()
 
@@ -252,7 +285,7 @@
 
     def fill_table(i, carry):
         row = order[i]
-        length = lengths_ref[row]
+        length = lengths_ref[0, row]
         for t in range(1, slots):
             column = columns_ref[t, row]
             place = jnp.where(column < bdev, inverse[jnp.minimum(column, bdev - 1)], column)
@@ -296,6 +329,77 @@
 
     lane = lax.broadcasted_iota(jnp.int32, (1, width), 1)
 
+    def to_natural(k, field):
+        local[...] = field
+        for r in range(bdev):
+            natural[k, r : r + 1, :] = local[pl.ds(inverse[r], 1), :]
+
+    def one_hot():
+        block = lax.broadcasted_iota(jnp.int32, (blank, bdev), 0)
+        pieces = [
+            jnp.where(
+                (block == columns_v[t : t + 1, :]) & (lengths_v[...] > t), 1.0, 0.0
+            )
+            for t in range(1, slots)
+        ]
+        return jnp.concatenate(pieces, axis=1).astype(jnp.bfloat16)
+
+    def transposed_product(i):
+        sums = [[] for _ in range(slots)]
+        for g in range(0, bdev, TILE):
+            parts = [[] for _ in range(slots)]
+            for r in range(g, g + TILE):
+                turned = jnp.broadcast_to(natural[i, r : r + 1, :], (width, width)).T
+                for t in range(slots):
+                    parts[t].append(
+                        total(
+                            [
+                                a[r, t, k : k + TILE, :] * turned[k : k + TILE, :]
+                                for k in range(0, width, TILE)
+                            ]
+                        )
+                    )
+            for t in range(slots):
+                sums[t].append(merge_rows(parts[t]))
+        others = jnp.concatenate([p for t in range(1, slots) for p in sums[t]], axis=0)
+        high = others.astype(jnp.bfloat16)
+        low = (others - high.astype(jnp.float32)).astype(jnp.bfloat16)
+        hot = one_hot()
+        spread = total(
+            [
+                lax.dot_general(
+                    hot,
+                    half,
+                    (((1,), (0,)), ((), ())),
+                    preferred_element_type=jnp.float32,
+                )
+                for half in (high, low)
+            ]
+        )
+        z[i, 0:bdev, :] = spread[0:bdev] + jnp.concatenate(sums[0], axis=0)
+        z[i, bdev:, :] = spread[bdev:]
+        for copy in z_copies(i):
+            copy.start()
+
+    def closing_dots(row, fields):
+        e = EXCHANGES - 1
+        last = len(fields)
+        for i, field in enumerate(fields):
+            terms = [
+                (shifted * field) * fields[-1],
+                z[i, 0:bdev, :] * natural[last - 1] * (-1.0 / SCALE),
+            ]
+            sums = [total([t[k : k + TILE] for k in range(0, bdev, TILE)]) for t in terms]
+            pieces = [z[i, bdev + q * gmax : bdev + (q + 1) * gmax, :] * extended[e][
+                bdev + q * gmax : bdev + (q + 1) * gmax, :
+            ] for q in range(UP, sides)] + [w[i, q] * packets[e][q] for q in range(UP)]
+            other = total([p[k : k + TILE] for p in pieces for k in range(0, gmax, TILE)])
+            folded = total(sums) - other * (1.0 / SCALE)
+            folded = jnp.sum(folded, axis=0, keepdims=True)
+            value = jnp.sum(folded, axis=1, keepdims=True)
+            row = jnp.where(lane == last * (last + 1) // 2 + i, value, row)
+        return row
+
     def dots(row, fields, last):
         for i in range(last + 1):
             folded = jnp.sum(fields[i] * fields[last], axis=0, keepdims=True)
@@ -358,13 +462,14 @@
             rows = slice(start, start + gmax)
             part = known[rows] - scale * other_product(source, start, start + gmax)
             parts.append(part)
-            if e is not None:
-                extended[e][rows, :] = part
-                local[rows, :] = part
-                if start == 0:
-                    send_lead(e)
-        if e is not None:
+            extended[e][rows, :] = part
+            local[rows, :] = part
+            if start == 0 and e < EXCHANGES - 1:
+                send_lead(e)
+        if e < EXCHANGES - 1:
             send_rest(e)
+        else:
+            send_last()
         return jnp.concatenate(parts, axis=0)
 
     def known_part(field):
@@ -404,31 +509,35 @@
     fields = [start, field]
     row = jnp.zeros((1, width), jnp.float32)
     row = dots(dots(row, fields, 0), fields, 1)
+    to_natural(KRYLOV, base)
+    for i, known_field in enumerate(fields):
+        to_natural(i, known_field)
+        transposed_product(i)
     arrive(e)
     mixed[bdev:blank, :] = combine(
         s, [extended[2 + j][bdev:blank, :] for j in range(KRYLOV + 1)]
     )
-    source = mixed
-    for j in range(2, KRYLOV + 1):
-        e = KRYLOV + 1 + j
-        field = finish(e if j < KRYLOV else None, source, known, 1.0 / SCALE)
-        fields.append(field)
-        if j < KRYLOV:
-            row = dots(row, fields, j)
-            known = known_part(field)
-            arrive(e)
-            source = extended[e]
-    send_sums(1, dots(row, fields, KRYLOV))
+    field = finish(EXCHANGES - 1, mixed, known, 1.0 / SCALE)
+    fields.append(field)
+    to_natural(KRYLOV - 1, field)
+    transposed_product(KRYLOV - 1)
+    row = dots(row, fields, KRYLOV - 1)
+    for q in range(UP, sides):
+        remote(EXCHANGES - 1, q, 0, q, packets[EXCHANGES - 1].at[q]).wait_recv()
+    for i in range(KRYLOV):
+        for copy in z_copies(i):
+            copy.wait_recv()
+    send_sums(1, closing_dots(row, fields))
     d = restart_coefficients(gather_sums(1, KRYLOV + 1), substep)
-    local[...] = base + combine(d, fields[:KRYLOV])
-    for r in range(bdev):
-        y[r : r + 1, :] = local[pl.ds(inverse[r], 1), :]
+    y[...] = natural[KRYLOV] + combine(d, [natural[i] for i in range(KRYLOV)])
 
     for copy in first_copies():
         copy.wait_send()
-    for e in range(1, EXCHANGES):
+    for e in range(1, EXCHANGES - 1):
         for j in range(sides):
             copy_of(e, j).wait_send()
+    for copy in last_copies() + [c for i in range(KRYLOV) for c in z_copies(i)]:
+        copy.wait_send()
     for turn in range(RESTARTS):
         others = sums[turn].at[pl.ds(0, n - 1)]
         pltpu.make_async_copy(others, others, sum_send.at[turn]).wait()
@@ -453,11 +562,11 @@
             scratch_shapes=[
                 pltpu.SMEM((1,), f32),
                 pltpu.SMEM((slots, bdev), jnp.int32),
-                pltpu.SMEM((bdev,), jnp.int32),
+                pltpu.SMEM((1, bdev), jnp.int32),
                 pltpu.SMEM((sides, gmax), jnp.int32),
                 pltpu.VMEM((bdev, width), f32),
                 pltpu.VMEM((bdev, width), f32),
-                pltpu.SemaphoreType.DMA((6,)),
+                pltpu.SemaphoreType.DMA((8,)),
                 pltpu.SMEM((bdev,), jnp.int32),
                 pltpu.SMEM((bdev,), jnp.int32),
                 pltpu.SMEM((bdev * slots,), jnp.int32),
@@ -466,6 +575,13 @@
                 pltpu.VMEM((bdev, width), f32),
                 pltpu.VMEM((bdev, width), f32),
                 pltpu.VMEM((tall, width), f32),
+                pltpu.VMEM((slots, bdev), jnp.int32),
+                pltpu.VMEM((1, bdev), jnp.int32),
+                pltpu.VMEM((KRYLOV + 1, bdev, width), f32),
+                pltpu.VMEM((KRYLOV, tall - 8, width), f32),
+                pltpu.VMEM((KRYLOV, UP, gmax, width), f32),
+                pltpu.SemaphoreType.DMA((KRYLOV, UP)),
+                pltpu.SemaphoreType.DMA((KRYLOV, UP)),
             ]
             + [pltpu.VMEM((tall, width), f32)] * EXCHANGES
             + [pltpu.VMEM((sides, gmax, width), f32)] * EXCHANGES
@@ -479,9 +595,15 @@
                 pltpu.SemaphoreType.DMA((RESTARTS,)),
             ],
             compiler_params=pltpu.CompilerParams(
-                collective_id=0, has_side_effects=True, vmem_limit_bytes=20 << 20
+                collective_id=0, has_side_effects=True, vmem_limit_bytes=24 << 20
             ),
-        )(step, *[pltpu.with_memory_space_constraint(x, pltpu.HBM) for x in (columns.T, lengths, lists[0], c, r, values)])
+        )(
+            step,
+            *[
+                pltpu.with_memory_space_constraint(x, pltpu.HBM)
+                for x in (columns.T, lengths.reshape(1, -1), lists[0], c, r, values)
+            ],
+        )
 
     placed = (
         P("dom", None),

time: 47.9 us -> 45.5 us (0.950)
  Pallas kernels: 46.5 us -> 44.1 us
    pallas_call x1, Pallas kernels: 46.5 us -> 44.1 us  [shards(): pl.pallas_call(functools.partial(kernel, n), out_shape=jax.ShapeDtypeStru...]
where the time goes in v3:
time: 45.5 us; the launch traced here: 45.4 us
  Pallas kernels  44.1 us (97%)
  between operations  0.66 us (1%)
  local copies, waits for them, and re-layouts  0.61 us (1%)
    pallas_call x1, Pallas kernels, shards(): pl.pallas_call(functools.partial(kernel, n), out_shape=jax.ShapeDtypeStru...  44.1 us

profile of v3, /device:TPU:0, one launch (start us, length us, event | category | flops | bytes accessed | tf_op | source)
XLA Modules:
  0.0 45.4 jit_solution(15393964903811780772)
XLA Ops:
  0.7 44.1 %shard_map.73 = f32[32,128]{1,0:T(8,128)S(1)} custom-call(f32[1]{0:T(128)S(6)} %copy.9.refs_0_, s32[5,32]{1,0:T(8,128)} %bitcast.3, s32[1,32]{1,0:T(1,128)} %bitcast.5, s32[4,16]{1,0:T(4,128)} %bitcast.4, f32[32,128]{1,0:T(8,128)} %refs_4_.1, f32[32,128]{1,0:T(8,128)} %refs_5_.1, f32[32,5,128,128]{3,2,1,0:T(8,128)} %refs_6_.1), custom_call_target="tpu_custom_call" | custom-call | tf_op jit(solution)/shard_map/pallas_call | solution.py:557
  44.8 0.6 %copy.10 = f32[32,128]{1,0:T(8,128)} copy(f32[32,128]{1,0:T(8,128)S(1)} %shard_map.73) | data formatting | bytes 32768

commit v4 on v3

--- a/solution.py
+++ b/solution.py
@@ -131,8 +131,8 @@
     step_ref, columns_ref, lengths_ref, lists_ref, c_ref, r_ref = staged
     scratch = list(refs[14:])
     stage_sem, inverse, order, table, places, a, local, rates, mixed = scratch[:9]
-    columns_v, lengths_v, natural, z, w, w_send, w_recv = scratch[9:16]
-    scratch = scratch[16:]
+    columns_v, lengths_v, natural, z, w, closing, w_send, w_recv = scratch[9:17]
+    scratch = scratch[17:]
     extended = scratch[:EXCHANGES]
     packets = scratch[EXCHANGES : 2 * EXCHANGES]
     rest = scratch[2 * EXCHANGES :]
@@ -207,32 +207,35 @@
         for g in range(gmax):
             packets[e][j, g : g + 1, :] = local[pl.ds(places[q * gmax + g], 1), :]
 
-    def last_copies():
-        return [
-            remote(EXCHANGES - 1, q, OFFSETS[q], q, packets[EXCHANGES - 1].at[q])
-            for q in range(UP, sides)
-        ]
+    def last_copy(q):
+        return remote(EXCHANGES - 1, q, OFFSETS[q], q, packets[EXCHANGES - 1].at[q])
+
+    def z_copy(i, q):
+        return pltpu.make_async_remote_copy(
+            src_ref=z.at[i, pl.ds(bdev + q * gmax, gmax)],
+            dst_ref=w.at[i, q],
+            send_sem=w_send.at[i, q],
+            recv_sem=w_recv.at[i, q],
+            device_id=(lax.rem(me - OFFSETS[q] + n, n),),
+            device_id_type=pl.DeviceIdType.MESH,
+        )
+
+    def at_the_bottom(q):
+        return me + OFFSETS[q] < 0
+
+    def at_the_top(q):
+        return me - OFFSETS[q] >= n
 
     def send_last():
+        for q in range(sides):
+            pack(EXCHANGES - 1, q, q)
         for q in range(UP, sides):
-            pack(EXCHANGES - 1, q, q)
-        for copy in last_copies():
-            copy.start()
+            last_copy(q).start()
         for q in range(UP):
-            pack(EXCHANGES - 1, q, q)
-
-    def z_copies(i):
-        return [
-            pltpu.make_async_remote_copy(
-                src_ref=z.at[i, pl.ds(bdev + q * gmax, gmax)],
-                dst_ref=w.at[i, q],
-                send_sem=w_send.at[i, q],
-                recv_sem=w_recv.at[i, q],
-                device_id=(lax.rem(me - OFFSETS[q] + n, n),),
-                device_id_type=pl.DeviceIdType.MESH,
-            )
-            for q in range(UP)
-        ]
+
+            @pl.when(jnp.logical_not(at_the_bottom(q)))
+            def _():
+                last_copy(q).start()
 
     def send_rest(e):
         for j in range(1, sides):
@@ -250,10 +253,6 @@
     for q in range(sides):
         for g in range(gmax):
             packets[0][q, g : g + 1, :] = c_ref[pl.ds(lists_ref[q, g], 1), :]
-    pl.semaphore_wait(barrier, n - 1)
-    for copy in first_copies():
-        copy.start()
-
     def fill_inverse(row, carry):
         hit = jnp.int32(0)
         below = jnp.int32(0)
@@ -264,15 +263,11 @@
         inverse[row] = jnp.where(hit > 0, hit - 1, gmax + row - below)
         return carry
 
-    lax.fori_loop(0, bdev, fill_inverse, 0)
-
     def fill_lead(i, carry):
         order[i] = lists_ref[lead, i]
         for q in range(sides):
             places[q * gmax + i] = inverse[lists_ref[q, i]]
         return carry
-
-    lax.fori_loop(0, gmax, fill_lead, 0)
 
     def fill_others(i, carry):
         row = jnp.int32(0)
@@ -280,8 +275,6 @@
             row = row + jnp.where(inverse[r] == i, r, 0)
         order[i] = row
         return carry
-
-    lax.fori_loop(gmax, bdev, fill_others, 0)
 
     def fill_table(i, carry):
         row = order[i]
@@ -292,7 +285,23 @@
             table[i * slots + t] = jnp.where(t < length, place, blank)
         return carry
 
-    lax.fori_loop(0, bdev, fill_table, 0)
+    def tables():
+        lax.fori_loop(0, bdev, fill_inverse, 0)
+        lax.fori_loop(0, gmax, fill_lead, 0)
+        lax.fori_loop(gmax, bdev, fill_others, 0)
+        lax.fori_loop(0, bdev, fill_table, 0)
+
+    @pl.when(2 * me < n)
+    def _():
+        tables()
+
+    pl.semaphore_wait(barrier, n - 1)
+    for copy in first_copies():
+        copy.start()
+
+    @pl.when(2 * me >= n)
+    def _():
+        tables()
 
     def rowsum(products):
         turned = products.T
@@ -378,23 +387,48 @@
         )
         z[i, 0:bdev, :] = spread[0:bdev] + jnp.concatenate(sums[0], axis=0)
         z[i, bdev:, :] = spread[bdev:]
-        for copy in z_copies(i):
-            copy.start()
+        for q in range(UP):
+
+            @pl.when(at_the_top(q))
+            def _():
+                z_copy(i, q).start()
+
+    def fold(field):
+        return total([field[k : k + TILE] for k in range(0, field.shape[0], TILE)])
 
     def closing_dots(row, fields):
         e = EXCHANGES - 1
         last = len(fields)
+        minus = -1.0 / SCALE
+
+        def ghosts(i, q):
+            rows = slice(bdev + q * gmax, bdev + (q + 1) * gmax)
+            return fold(z[i, rows, :] * extended[e][rows, :])
+
+        def arrived(q):
+            remote(e, q, 0, q, packets[e].at[q]).wait_recv()
+
         for i, field in enumerate(fields):
-            terms = [
-                (shifted * field) * fields[-1],
-                z[i, 0:bdev, :] * natural[last - 1] * (-1.0 / SCALE),
-            ]
-            sums = [total([t[k : k + TILE] for k in range(0, bdev, TILE)]) for t in terms]
-            pieces = [z[i, bdev + q * gmax : bdev + (q + 1) * gmax, :] * extended[e][
-                bdev + q * gmax : bdev + (q + 1) * gmax, :
-            ] for q in range(UP, sides)] + [w[i, q] * packets[e][q] for q in range(UP)]
-            other = total([p[k : k + TILE] for p in pieces for k in range(0, gmax, TILE)])
-            folded = total(sums) - other * (1.0 / SCALE)
+            own = fold(z[i, 0:bdev, :] * natural[last - 1])
+            closing[i] = fold((shifted * field) * fields[-1]) + own * minus
+        for q in range(UP):
+
+            @pl.when(at_the_bottom(q))
+            def _():
+                for i in range(last):
+                    z_copy(i, q).wait_recv()
+                    closing[i] = closing[i] + fold(w[i, q] * packets[e][q]) * minus
+
+            @pl.when(jnp.logical_not(at_the_top(q)))
+            def _():
+                arrived(q)
+                for i in range(last):
+                    closing[i] = closing[i] + ghosts(i, q) * minus
+
+        for q in range(UP, sides):
+            arrived(q)
+        for i in range(last):
+            folded = closing[i] + total([ghosts(i, q) for q in range(UP, sides)]) * minus
             folded = jnp.sum(folded, axis=0, keepdims=True)
             value = jnp.sum(folded, axis=1, keepdims=True)
             row = jnp.where(lane == last * (last + 1) // 2 + i, value, row)
@@ -522,11 +556,6 @@
     to_natural(KRYLOV - 1, field)
     transposed_product(KRYLOV - 1)
     row = dots(row, fields, KRYLOV - 1)
-    for q in range(UP, sides):
-        remote(EXCHANGES - 1, q, 0, q, packets[EXCHANGES - 1].at[q]).wait_recv()
-    for i in range(KRYLOV):
-        for copy in z_copies(i):
-            copy.wait_recv()
     send_sums(1, closing_dots(row, fields))
     d = restart_coefficients(gather_sums(1, KRYLOV + 1), substep)
     y[...] = natural[KRYLOV] + combine(d, [natural[i] for i in range(KRYLOV)])
@@ -536,8 +565,19 @@
     for e in range(1, EXCHANGES - 1):
         for j in range(sides):
             copy_of(e, j).wait_send()
-    for copy in last_copies() + [c for i in range(KRYLOV) for c in z_copies(i)]:
-        copy.wait_send()
+    for q in range(UP, sides):
+        last_copy(q).wait_send()
+    for q in range(UP):
+
+        @pl.when(jnp.logical_not(at_the_bottom(q)))
+        def _():
+            last_copy(q).wait_send()
+
+        @pl.when(at_the_top(q))
+        def _():
+            for i in range(KRYLOV):
+                z_copy(i, q).wait_send()
+
     for turn in range(RESTARTS):
         others = sums[turn].at[pl.ds(0, n - 1)]
         pltpu.make_async_copy(others, others, sum_send.at[turn]).wait()
@@ -580,6 +620,7 @@
                 pltpu.VMEM((KRYLOV + 1, bdev, width), f32),
                 pltpu.VMEM((KRYLOV, tall - 8, width), f32),
                 pltpu.VMEM((KRYLOV, UP, gmax, width), f32),
+                pltpu.VMEM((KRYLOV, TILE, width), f32),
                 pltpu.SemaphoreType.DMA((KRYLOV, UP)),
                 pltpu.SemaphoreType.DMA((KRYLOV, UP)),
             ]

time: 45.5 us -> 44.6 us (0.980)
  Pallas kernels: 44.1 us -> 43.2 us
    pallas_call x1, Pallas kernels: 44.1 us -> 43.2 us  [shards(): pl.pallas_call(functools.partial(kernel, n), out_shape=jax.ShapeDtypeStru...]
where the time goes in v4:
time: 44.6 us; the launch traced here: 44.4 us
  Pallas kernels  43.2 us (97%)
  between operations  0.66 us (1%)
  local copies, waits for them, and re-layouts  0.61 us (1%)
    pallas_call x1, Pallas kernels, shards(): pl.pallas_call(functools.partial(kernel, n), out_shape=jax.ShapeDtypeStru...  43.2 us

profile of v4, /device:TPU:0, one launch (start us, length us, event | category | flops | bytes accessed | tf_op | source)
XLA Modules:
  0.0 44.4 jit_solution(1111079792671895375)
XLA Ops:
  0.7 43.2 %shard_map.73 = f32[32,128]{1,0:T(8,128)S(1)} custom-call(f32[1]{0:T(128)S(6)} %copy.9.refs_0_, s32[5,32]{1,0:T(8,128)} %bitcast.3, s32[1,32]{1,0:T(1,128)} %bitcast.5, s32[4,16]{1,0:T(4,128)} %bitcast.4, f32[32,128]{1,0:T(8,128)} %refs_4_.1, f32[32,128]{1,0:T(8,128)} %refs_5_.1, f32[32,5,128,128]{3,2,1,0:T(8,128)} %refs_6_.1), custom_call_target="tpu_custom_call" | custom-call | tf_op jit(solution)/shard_map/pallas_call | solution.py:597
  43.8 0.6 %copy.10 = f32[32,128]{1,0:T(8,128)} copy(f32[32,128]{1,0:T(8,128)S(1)} %shard_map.73) | data formatting | bytes 32768

commit v5 on v4

--- a/solution.py
+++ b/solution.py
@@ -132,7 +132,8 @@
     scratch = list(refs[14:])
     stage_sem, inverse, order, table, places, a, local, rates, mixed = scratch[:9]
     columns_v, lengths_v, natural, z, w, closing, w_send, w_recv = scratch[9:17]
-    scratch = scratch[17:]
+    relay, relay_send, relay_recv, back, ahead, spread_sem = scratch[17:23]
+    scratch = scratch[23:]
     extended = scratch[:EXCHANGES]
     packets = scratch[EXCHANGES : 2 * EXCHANGES]
     rest = scratch[2 * EXCHANGES :]
@@ -147,14 +148,27 @@
 
     barrier = pltpu.get_barrier_semaphore()
 
-    def greet(d, carry):
+    odd = lax.rem(me, 2) == 1
+    even = jnp.logical_not(odd)
+
+    def signal(semaphore, d):
         pl.semaphore_signal(
-            barrier,
+            semaphore,
             inc=1,
-            device_id=(lax.rem(me + d, n),),
+            device_id=(lax.rem(me + d + n, n),),
             device_id_type=pl.DeviceIdType.MESH,
         )
-        return carry
+
+    signal(barrier, -2)
+
+    @pl.when(even)
+    def _():
+        signal(barrier, 1)
+        signal(barrier, -1)
+
+    @pl.when(me == 1)
+    def _():
+        signal(barrier, -3)
 
     stages = [
         pltpu.make_async_copy(source, target, stage_sem.at[i])
@@ -164,15 +178,36 @@
     ]
     for copy in stages:
         copy.start()
-    lax.fori_loop(1, n, greet, 0)
+    @pl.when(odd)
+    def _():
+        pl.semaphore_wait(barrier, 3)
+        signal(back.at[0], 2)
+        signal(back.at[2], -1)
+
+        @pl.when(me != n - 1)
+        def _():
+            signal(back.at[1], 1)
+
+    @pl.when(even)
+    def _():
+        pl.semaphore_wait(barrier, 1 + (me == n - 2).astype(jnp.int32))
+
+        @pl.when(me != n - 2)
+        def _():
+            signal(back.at[0], 2)
+
+        @pl.when(me == n - 2)
+        def _():
+            signal(ahead.at[0], 3)
+
+    for copy in stages:
+        copy.wait()
     loads = []
     for g in range(0, bdev, TILE):
         rows = pl.ds(g, TILE)
         copy = pltpu.make_async_copy(a_ref.at[rows], a.at[rows], load_sem.at[g // TILE])
         copy.start()
         loads.append(copy)
-    for copy in stages:
-        copy.wait()
 
     lead = (sides - 1) * lax.div(2 * me, n)
 
@@ -190,10 +225,28 @@
             device_id_type=pl.DeviceIdType.MESH,
         )
 
-    def first_copies():
-        return [
-            remote(0, q, offset, q, packets[0].at[q]) for q, offset in enumerate(OFFSETS)
-        ]
+    def first_copy(q):
+        return remote(0, q, OFFSETS[q], q, packets[0].at[q])
+
+    def relay_in(q):
+        return pltpu.make_async_remote_copy(
+            src_ref=packets[0].at[q],
+            dst_ref=relay.at[q],
+            send_sem=send_sem.at[0, q],
+            recv_sem=relay_recv.at[q],
+            device_id=(lax.rem(me + 1, n),),
+            device_id_type=pl.DeviceIdType.MESH,
+        )
+
+    def relay_out(q):
+        return pltpu.make_async_remote_copy(
+            src_ref=relay.at[q],
+            dst_ref=extended[0].at[pl.ds(bdev + q * gmax, gmax)],
+            send_sem=relay_send.at[q],
+            recv_sem=recv_sem.at[0, q],
+            device_id=(lax.rem(me - 1 + OFFSETS[q] + n, n),),
+            device_id_type=pl.DeviceIdType.MESH,
+        )
 
     def copy_of(e, j):
         q, offset = side(j)
@@ -291,15 +344,46 @@
         lax.fori_loop(gmax, bdev, fill_others, 0)
         lax.fori_loop(0, bdev, fill_table, 0)
 
-    @pl.when(2 * me < n)
+    @pl.when(me < 2)
     def _():
         tables()
 
-    pl.semaphore_wait(barrier, n - 1)
-    for copy in first_copies():
-        copy.start()
-
-    @pl.when(2 * me >= n)
+
+    @pl.when(odd)
+    def _():
+        first_copy(3).start()
+        first_copy(1).start()
+        first_copy(2).start()
+        pl.semaphore_wait(back.at[0], 1)
+        first_copy(0).start()
+
+    @pl.when(even)
+    def _():
+        first_copy(3).start()
+        pl.semaphore_wait(back.at[2], 1)
+        first_copy(2).start()
+
+        @pl.when(me == 0)
+        def _():
+            for q in range(UP):
+                relay_in(q).start()
+
+        @pl.when(me != 0)
+        def _():
+            pl.semaphore_wait(back.at[1], 1)
+            first_copy(1).start()
+            pl.semaphore_wait(back.at[0], 1)
+            first_copy(0).start()
+
+    @pl.when(me == 1)
+    def _():
+        for q in range(UP):
+            relay_in(q).wait_recv()
+        pl.semaphore_wait(ahead.at[0], 1)
+        for q in range(UP):
+            relay_out(q).start()
+
+    @pl.when(me >= 2)
     def _():
         tables()
 
@@ -516,9 +600,25 @@
     arrive(0)
     field = finish(1, extended[0], known, 1.0)
 
+    reaches = [2]
+    while 4 * reaches[-1] < n:
+        reaches.append(2 * reaches[-1])
+
+    def heard(k):
+        pl.semaphore_wait(spread_sem.at[k], 2)
+
+    def spread(start, stop):
+        for k in range(start, min(stop, len(reaches))):
+            if k:
+                heard(k - 1)
+            signal(spread_sem.at[k], reaches[k])
+            signal(spread_sem.at[k], -reaches[k])
+
+    share = -(-len(reaches) // KRYLOV)
     fields = [field]
     row = jnp.zeros((1, width), jnp.float32)
     for j in range(KRYLOV):
+        spread(j * share, (j + 1) * share)
         row = dots(row, fields, j)
         known = known_part(field)
         arrive(1 + j)
@@ -526,6 +626,7 @@
         fields.append(field)
 
     e = KRYLOV + 1
+    heard(len(reaches) - 1)
     send_sums(0, dots(row, fields, KRYLOV))
     known = known_part(field)
     arrive(e)
@@ -560,8 +661,14 @@
     d = restart_coefficients(gather_sums(1, KRYLOV + 1), substep)
     y[...] = natural[KRYLOV] + combine(d, [natural[i] for i in range(KRYLOV)])
 
-    for copy in first_copies():
-        copy.wait_send()
+    for q in range(sides):
+        first_copy(q).wait_send()
+
+    @pl.when(me == 1)
+    def _():
+        for q in range(UP):
+            relay_out(q).wait_send()
+
     for e in range(1, EXCHANGES - 1):
         for j in range(sides):
             copy_of(e, j).wait_send()
@@ -623,6 +730,12 @@
                 pltpu.VMEM((KRYLOV, TILE, width), f32),
                 pltpu.SemaphoreType.DMA((KRYLOV, UP)),
                 pltpu.SemaphoreType.DMA((KRYLOV, UP)),
+                pltpu.VMEM((UP, gmax, width), f32),
+                pltpu.SemaphoreType.DMA((UP,)),
+                pltpu.SemaphoreType.DMA((UP,)),
+                pltpu.SemaphoreType.REGULAR((UP + 1,)),
+                pltpu.SemaphoreType.REGULAR((1,)),
+                pltpu.SemaphoreType.REGULAR((n.bit_length(),)),
             ]
             + [pltpu.VMEM((tall, width), f32)] * EXCHANGES
             + [pltpu.VMEM((sides, gmax, width), f32)] * EXCHANGES

time: 44.6 us -> 44.3 us (level)
  no operation moved by 1% of the time
where the time goes in v5:
time: 44.3 us; the launch traced here: 44.2 us
  Pallas kernels  42.9 us (97%)
  between operations  0.66 us (1%)
  local copies, waits for them, and re-layouts  0.61 us (1%)
    pallas_call x1, Pallas kernels, shards(): pl.pallas_call(functools.partial(kernel, n), out_shape=jax.ShapeDtypeStru...  42.9 us

profile of v5, /device:TPU:0, one launch (start us, length us, event | category | flops | bytes accessed | tf_op | source)
XLA Modules:
  0.0 44.2 jit_solution(16181919537766799385)
XLA Ops:
  0.7 42.9 %shard_map.73 = f32[32,128]{1,0:T(8,128)S(1)} custom-call(f32[1]{0:T(128)S(6)} %copy.9.refs_0_, s32[5,32]{1,0:T(8,128)} %bitcast.3, s32[1,32]{1,0:T(1,128)} %bitcast.5, s32[4,16]{1,0:T(4,128)} %bitcast.4, f32[32,128]{1,0:T(8,128)} %refs_4_.1, f32[32,128]{1,0:T(8,128)} %refs_5_.1, f32[32,5,128,128]{3,2,1,0:T(8,128)} %refs_6_.1), custom_call_target="tpu_custom_call" | custom-call | tf_op jit(solution)/shard_map/pallas_call | solution.py:704
  43.6 0.6 %copy.10 = f32[32,128]{1,0:T(8,128)} copy(f32[32,128]{1,0:T(8,128)S(1)} %shard_map.73) | data formatting | bytes 32768
